TPU v7x, 256 devices: a whole 4x4x8 slice. The times are simulated.
256 devices in a mesh: feat: 8 (over x, core), rows: 32 (over z, y).
Axes of the slice: x: 4, y: 4, z: 8, core: 2. Of those that a mesh axis runs over, the one named last changes fastest.
Arguments:
- acts: bfloat16 [32768, 16384], P('rows', 'feat'), may hold values from -6 to 6
- grads_out: bfloat16 [32768, 16384], P('rows', 'feat'), may hold values from -0.59765625 to 0.59765625
- proj_in: bfloat16 [16384, 128], P('feat'), may hold values from -0.046875 to 0.046875
- proj_out: bfloat16 [16384, 128], P('feat'), may hold values from -0.046875 to 0.046875
- doc_ids: int32 [32768], P('rows'), may hold values from -1 to 127, as said below
- block_counts: int32 [128], replicated, may hold values from 1 to 65, as said below
- inverse_dense: bfloat16 [16384, 16384], P('rows', 'feat'), may hold values from -0.046875 to 0.046875
- inverse_diag: float32 [16384], P('rows'), may hold values from 0.5 to 2
- train_grads: bfloat16 [16384, 16384], P('rows', 'feat'), may hold values from -0.046875 to 0.046875
Outputs:
- scores: float32 [128, 16384], P('feat', 'rows')
Inputs may be any that keep to these rules, and one draw needn't show every extreme that they name: `doc_ids`: documents are laid end to end in order, document d over block_counts_d whole blocks of 128 tokens; its tokens come first and the rest of its last block is padding with id -1; every block holds real tokens of its document. `block_counts`: the counts sum to 256; one document has exactly the most.
All inputs are finite; a program needn't handle non-finite values.
Results may differ from a plain program's by a relative error of at most 0.0057.
Values may be sent and summed in bfloat16 or wider, within the bound.
A program may use at most 64 MiB of HBM per device.

v0:
```python
import jax
import jax.numpy as jnp
from jax import lax
from jax.sharding import PartitionSpec as P

BLOCK = 128


def split_up(value, dim, length):
    shape = value.shape
    blocks = value.reshape(*shape[:dim], length, shape[dim] // length, *shape[dim + 1 :])
    return jnp.moveaxis(blocks, dim, 0)


def sent_and_summed(value, axis, dim):
    blocks = split_up(value, dim, lax.axis_size(axis))
    arrived = lax.all_to_all(blocks, axis, split_axis=0, concat_axis=0, tiled=True)
    return arrived.sum(axis=0)


def sent_together(arrays, axis, dim, along):
    widths = [a.shape[along] for a in arrays]
    both = jnp.concatenate(arrays, axis=along)
    filled = sent_and_summed(both, axis, dim)
    return tuple(jnp.split(filled, [sum(widths[:k]) for k in range(1, len(widths))], axis=along))


def in_one_piece(arrays, axis, dim, along):
    both = jnp.concatenate(arrays, axis=along)
    filled, at, gathered = (lax.all_gather(both, axis, axis=dim, tiled=True), 0, [])
    for a in arrays:
        gathered.append(lax.slice_in_dim(filled, at, at + a.shape[along], axis=along))
        at += a.shape[along]
    return tuple(gathered)


def from_everyone(value, axis):
    copies = jnp.broadcast_to(value, (lax.axis_size(axis), *value.shape))
    return lax.all_to_all(copies, axis, split_axis=0, concat_axis=0, tiled=True)


def joined_along(blocks, dim):
    shape = list(blocks.shape[1:])
    shape[dim] *= blocks.shape[0]
    return jnp.moveaxis(blocks, 0, dim).reshape(shape)


def collect(value, axis, dim):
    blocks = from_everyone(value, axis)
    return joined_along(blocks, dim)


def owners(block_counts, total_blocks):
    starts = jnp.cumsum(block_counts) - block_counts
    places = jnp.arange(total_blocks, dtype=jnp.int32)
    return jnp.sum((starts[None, :] <= places[:, None]).astype(jnp.int32), axis=1) - 1


def per_device(
    acts,
    grads_out,
    proj_in,
    proj_out,
    doc_ids,
    block_counts,
    inverse_dense,
    inverse_diag,
    train_grads,
):
    tok_rows = acts.shape[0]
    row_count = lax.axis_size("rows")
    feat_count = lax.axis_size("feat")
    row_index = lax.axis_index("rows")
    feat_index = lax.axis_index("feat")
    part_in = jnp.dot(acts, proj_in, preferred_element_type=jnp.float32)
    part_out = jnp.dot(grads_out, proj_out, preferred_element_type=jnp.float32)
    share_in, share_out = sent_together((part_in, part_out), "feat", 0, 1)
    xin, gout = in_one_piece(
        (share_in.astype(jnp.bfloat16), share_out.astype(jnp.bfloat16)), "feat", 0, 1
    )
    width = xin.shape[1]
    doc_count = block_counts.shape[0]
    local_blocks = tok_rows // BLOCK
    total_blocks = local_blocks * row_count
    owner = owners(block_counts, total_blocks)
    local_owner = lax.dynamic_slice_in_dim(owner, row_index * local_blocks, local_blocks, 0)
    tok_owner = jnp.repeat(local_owner, BLOCK)
    gmask = jnp.where((doc_ids == tok_owner)[:, None], gout, jnp.zeros_like(gout))
    local_sums = jnp.einsum(
        "kta,ktc->kac",
        gmask.reshape(local_blocks, BLOCK, width),
        xin.reshape(local_blocks, BLOCK, width),
        preferred_element_type=jnp.float32,
    ).reshape(local_blocks, width * width)
    blocksum = lax.all_to_all(local_sums, "rows", split_axis=1, concat_axis=0, tiled=True)
    member = (owner[None, :] == jnp.arange(doc_count, dtype=jnp.int32)[:, None]).astype(jnp.float32)
    summed = jnp.dot(member, blocksum, precision=lax.Precision.HIGHEST)
    docgrad = (summed / block_counts.astype(jnp.float32)[:, None]).astype(jnp.bfloat16)
    dense = jnp.dot(docgrad, inverse_dense, preferred_element_type=jnp.float32)
    ratio = row_count // feat_count
    row_width = docgrad.shape[1]
    diag_term = docgrad.astype(jnp.float32) * inverse_diag[None, :]
    placed = lax.dynamic_update_slice(
        jnp.zeros(dense.shape, jnp.float32),
        diag_term,
        (jnp.int32(0), row_index % ratio * row_width),
    )
    dense = dense + jnp.where(row_index // ratio == feat_index, placed, jnp.zeros_like(placed))
    shares = sent_and_summed(dense, "rows", 0).astype(jnp.bfloat16)
    precond = collect(shares, "rows", 0)
    partial_scores = lax.dot_general(
        precond, train_grads, (((1,), (1,)), ((), ())), preferred_element_type=jnp.float32
    )
    return sent_and_summed(partial_scores, "feat", 0)


def solution(mesh):
    in_specs = (
        P("rows", "feat"),
        P("rows", "feat"),
        P("feat", None),
        P("feat", None),
        P("rows"),
        P(),
        P("rows", "feat"),
        P("rows"),
        P("rows", "feat"),
    )
    out_specs = P("feat", "rows")
    return jax.shard_map(
        per_device, mesh=mesh, in_specs=in_specs, out_specs=out_specs, check_vma=False
    )
```

profile of v0, /device:TPU:1, one launch (start us, length us, event | category | flops | bytes accessed | tf_op | source)
XLA Modules:
  0.0 142.2 jit_solution(17568814523730681517)
XLA Ops:
  0.0 4.0 %fusion.7 = f32[1024,128]{0,1:T(8,128)S(1)} fusion(bf16[1024,2048]{1,0:T(8,128)(2,1)} %param.9, bf16[2048,128]{1,0:T(8,128)(2,1)} %param.11), kind=kOutput, calls=%fused_computation.17 | convolution fusion | flops 536870912 | bytes 5242880 | tf_op jit(solution)/shard_map/dot_general | solution.py:75
  4.0 1.5 %fusion.8 = f32[1024,128]{0,1:T(8,128)S(1)} fusion(bf16[1024,2048]{1,0:T(8,128)(2,1)S(1)} %copy-done.1, bf16[2048,128]{1,0:T(8,128)(2,1)S(1)} %copy-done.2), kind=kOutput, calls=%fused_computation.18 | convolution fusion | flops 536870912 | bytes 5242880 | tf_op jit(solution)/shard_map/dot_general | solution.py:76
  5.6 1.1 copy_bitcast_fusion
  6.6 6.6 %all-to-all-start = ((f32[8,128,256]{1,2,0:T(8,128)}), f32[8,128,256]{1,2,0:T(8,128)S(1)}, u32[]{:S(2)}, u32[]{:S(2)}) async-start(f32[8,128,256]{1,2,0:T(8,128)} %copy_bitcast_fusion), calls=%async_computation | async-start | bytes 2097152 | tf_op jit(solution)/shard_map/all_to_all | solution.py:17
  13.4 0.2 reduce-window.9
  13.7 0.1 convert_reduce_fusion
  14.0 14.3 %all-to-all-done = f32[8,128,256]{1,2,0:T(8,128)S(1)} async-done(((f32[8,128,256]{1,2,0:T(8,128)}), f32[8,128,256]{1,2,0:T(8,128)S(1)}, u32[]{:S(2)}, u32[]{:S(2)}) %all-to-all-start) | async-done | bytes 1048608 | tf_op jit(solution)/shard_map/all_to_all | solution.py:17
  28.3 13.0 %all_gather.3 = bf16[1024,256]{0,1:T(8,128)(2,1)S(1)} all-gather(bf16[128,256]{0,1:T(8,128)(2,1)S(1)} %reduce_sum.37), channel_id=1, replica_groups=mesh['feat'=8,'rows'=32] {'feat'}, dimensions={0}, use_global_device_ids=true | all-gather | bytes 589824 | tf_op jit(solution)/shard_map/all_gather | solution.py:30
  41.3 0.2 copy.25
  41.5 0.2 copy.24
  41.7 0.3 fusion.9
  42.1 1.1 copy.27
  43.2 10.3 %all-to-all-start.1 = ((f32[8,32,512]{2,0,1:T(8,128)}), f32[8,32,512]{2,0,1:T(8,128)S(1)}, u32[]{:S(2)}, u32[]{:S(2)}) async-start(f32[8,32,512]{2,0,1:T(8,128)} %copy.27), calls=%async_computation.1 | async-start | bytes 1048576 | tf_op jit(solution)/shard_map/all_to_all | solution.py:95
  53.5 16.7 %all-to-all-done.1 = f32[8,32,512]{2,0,1:T(8,128)S(1)} async-done(((f32[8,32,512]{2,0,1:T(8,128)}), f32[8,32,512]{2,0,1:T(8,128)S(1)}, u32[]{:S(2)}, u32[]{:S(2)}) %all-to-all-start.1) | async-done | bytes 524320 | tf_op jit(solution)/shard_map/all_to_all | solution.py:95
  70.2 0.3 fusion.2
  70.5 0.4 fusion.10
  71.1 1.3 reshape.63
  72.4 30.9 %all_to_all.39 = f32[32,4,2048]{2,1,0:T(4,128)S(1)} all-to-all(f32[32,4,2048]{2,1,0:T(4,128)} %reshape.63), channel_id=1, replica_groups=mesh['feat'=8,'rows'=32] {'rows'}, dimensions={0} | all-to-all | bytes 2097152 | tf_op jit(solution)/shard_map/all_to_all | solution.py:17
  103.3 0.2 reduce_sum.38
  103.4 0.2 broadcast_in_dim.27
  103.7 21.1 %all_to_all.40 = bf16[32,4,2048]{2,1,0:T(4,128)(2,1)S(1)} all-to-all(bf16[32,4,2048]{2,1,0:T(4,128)(2,1)S(1)} %broadcast_in_dim.27), channel_id=1, replica_groups=mesh['feat'=8,'rows'=32] {'rows'}, dimensions={0} | all-to-all | bytes 1048576 | tf_op jit(solution)/shard_map/all_to_all | solution.py:39
  124.9 2.4 %fusion = f32[8,16,512]{2,1,0:T(8,128)S(1)} fusion(bf16[8,16,2048]{2,1,0:T(8,128)(2,1)S(1)} %dot_general.28, bf16[512,2048]{1,0:T(8,128)(2,1)} %param.17), kind=kOutput, calls=%fused_computation | convolution fusion | flops 268435456 | bytes 2883584 | tf_op jit(solution)/shard_map/dot_general | solution.py:111
  127.3 14.3 %all_to_all.41 = f32[8,16,512]{2,1,0:T(8,128)S(1)} all-to-all(f32[8,16,512]{2,1,0:T(8,128)S(1)} %fusion), channel_id=1, replica_groups=mesh['feat'=8,'rows'=32] {'feat'}, dimensions={0} | all-to-all | bytes 524288 | tf_op jit(solution)/shard_map/all_to_all | solution.py:17
  141.6 0.6 reduce_sum.39
  (23 shorter events, 0.8 us)
Async XLA Ops:
  0.0 70.5 %copy-start = (bf16[512,2048]{1,0:T(8,128)(2,1)S(1)}, bf16[512,2048]{1,0:T(8,128)(2,1)}, u32[]{:S(2)}) copy-start(bf16[512,2048]{1,0:T(8,128)(2,1)} %param.15) | copy-start | bytes 6291460
  0.0 4.0 %copy-start.2 = (bf16[2048,128]{1,0:T(8,128)(2,1)S(1)}, bf16[2048,128]{1,0:T(8,128)(2,1)}, u32[]{:S(2)}) copy-start(bf16[2048,128]{1,0:T(8,128)(2,1)} %param.12) | copy-start | bytes 1572868
  0.0 4.0 %copy-start.1 = (bf16[1024,2048]{1,0:T(8,128)(2,1)S(1)}, bf16[1024,2048]{1,0:T(8,128)(2,1)}, u32[]{:S(2)}) copy-start(bf16[1024,2048]{1,0:T(8,128)(2,1)} %param.10) | copy-start | bytes 12582916
  4.0 9.3 %copy-start.5 = (s32[128]{0:T(128)S(1)}, s32[128]{0:T(128)}, u32[]{:S(2)}) copy-start(s32[128]{0:T(128)} %param.14) | copy-start | bytes 1540
  4.0 9.9 %copy-start.3 = (s32[1024]{0:T(1024)S(1)}, s32[1024]{0:T(1024)}, u32[]{:S(2)}) copy-start(s32[1024]{0:T(1024)} %param.13) | copy-start | bytes 12292
  6.6 21.6 %all-to-all-start = ((f32[8,128,256]{1,2,0:T(8,128)}), f32[8,128,256]{1,2,0:T(8,128)S(1)}, u32[]{:S(2)}, u32[]{:S(2)}) async-start(f32[8,128,256]{1,2,0:T(8,128)} %copy_bitcast_fusion), calls=%async_computation | async-start | bytes 2097152 | tf_op jit(solution)/shard_map/all_to_all | solution.py:17
  41.7 29.3 %copy-start.4 = (f32[512]{0:T(512)S(1)}, f32[512]{0:T(512)}, u32[]{:S(2)}) copy-start(f32[512]{0:T(512)} %param.16) | copy-start | bytes 6148
  43.2 27.0 %all-to-all-start.1 = ((f32[8,32,512]{2,0,1:T(8,128)}), f32[8,32,512]{2,0,1:T(8,128)S(1)}, u32[]{:S(2)}, u32[]{:S(2)}) async-start(f32[8,32,512]{2,0,1:T(8,128)} %copy.27), calls=%async_computation.1 | async-start | bytes 1048576 | tf_op jit(solution)/shard_map/all_to_all | solution.py:95
where the time goes:
time: 143 us; the launch traced here: 142 us
  blocking collectives  79.3 us (55%)
  waiting for transfers between devices  31 us (22%)
  starting transfers between devices  17 us (12%)
  matrix products  8.97 us (6%)
  local copies, waits for them, and re-layouts  3.38 us (2%)
  other arithmetic  2.48 us (2%)
    all_to_all x2, blocking collectives, sent_and_summed(): lax.all_to_all(blocks, axis, split_axis=0, concat_axis=0, tiled=True)  45.2 us
    all_to_all x1, blocking collectives, from_everyone(): return lax.all_to_all(copies, axis, split_axis=0, concat_axis=0, tiled=True)  21.1 us
    all_to_all x1, waiting for transfers between devices, per_device(): lax.all_to_all(local_sums, 'rows', split_axis=1, concat_axis=0, tiled=True)  16.7 us
    all_to_all x1, waiting for transfers between devices, sent_and_summed(): lax.all_to_all(blocks, axis, split_axis=0, concat_axis=0, tiled=True)  14.3 us
    all_gather x1, blocking collectives, in_one_piece(): lax.all_gather(both, axis, axis=dim, tiled=True)  13 us
    all_to_all x1, starting transfers between devices, per_device(): lax.all_to_all(local_sums, 'rows', split_axis=1, concat_axis=0, tiled=True)  10.3 us
    all_to_all x1, starting transfers between devices, sent_and_summed(): lax.all_to_all(blocks, axis, split_axis=0, concat_axis=0, tiled=True)  6.65 us
    dot_general x1, matrix products, per_device(): part_in = jnp.dot(acts, proj_in, preferred_element_type=jnp.float32)  3.97 us
  transfers between devices with their start and end apart: 2, of which 2 were waited for; matrix products, arithmetic and copies ran while one was open for 0% of the time, Pallas kernels for 0%

commit v1 on v0

v1 whole, which is shorter than its diff:
```python
import jax
import jax.numpy as jnp
from jax import lax
from jax.experimental import pallas as pl
from jax.experimental.pallas import tpu as pltpu
from jax.sharding import PartitionSpec as P

BF = jnp.bfloat16
F32 = jnp.float32
I32 = jnp.int32

NX, NC, NY, NZ = 4, 2, 4, 8
NF = NX * NC
NR = NZ * NY
BLOCK = 128
K = 128
DOCS = 128
X_ORDER = (2, 1, 3, 0)
Y_FAR = (2, 1, 3)
Y_NEAR = (1, 3, 2)
Z_FAR = (4, 3, 5, 2, 6, 1, 7)
Z_NEAR = (1, 7, 2, 6, 3, 5, 4)
F_FAR = (4, 5, 3, 2, 6, 7, 1)
X_DT = BF
D_DT = F32


def iota(shape, dim):
    return lax.broadcasted_iota(I32, shape, dim)


def one_hot_rows(source_of):
    q = iota((K, K), 0)
    return (iota((K, K), 1) == source_of(q)).astype(F32).astype(BF)


def dot(a, b):
    return jnp.dot(a, b, preferred_element_type=F32)


def dot_nt(a, b):
    return lax.dot_general(a, b, (((1,), (1,)), ((), ())), preferred_element_type=F32)


def kernel(
    acts, grads, pin, pout, ids, counts, inv, diag, train,
    out,
    acts_v, grads_v, pin_v, pout_v, ids_v, counts_v, inv_v, diag_v, train_v,
    member, perms, columns,
    pa, sib, xs, xr, s1, r1, s2, r2, ags, ag, dg, s3, r3, own, s4, r4, pc, acc, s5, r5,
    in_sem, chunk_sem,
    sib_send, sib_recv, x_send, x_recv, b1_send, b1_recv, b2_send, b2_recv,
    ag_send, ag_recv, c1_send, c1_recv, c2_send, c2_recv, p1_send, p1_recv,
    p2_send, p2_recv, d_send, d_recv,
):
    f = lax.axis_index("feat")
    r = lax.axis_index("rows")
    x, c = f // NC, f % NC
    z, y = r // NY, r % NY

    def feat_at(k):
        return {"feat": lax.rem(f + k, NF)}

    def y_at(k):
        return lax.rem(y + k, NY)

    def z_at(k):
        return lax.rem(z + k, NZ)

    def rows_peer(zp, yp):
        return {"rows": zp * NY + yp}

    sibling = {"feat": x * NC + (1 - c)}

    loads = [
        pltpu.make_async_copy(counts, counts_v, in_sem.at[0]),
        pltpu.make_async_copy(ids, ids_v, in_sem.at[1]),
        pltpu.make_async_copy(pin, pin_v, in_sem.at[2]),
        pltpu.make_async_copy(pout, pout_v, in_sem.at[3]),
    ]
    for copy in loads:
        copy.start()
    chunk = {}
    for k in X_ORDER:
        at = pl.ds(pl.multiple_of(lax.rem(x + k, NX) * 256, 256), 256)
        chunk[k] = (
            pltpu.make_async_copy(acts.at[at, :], acts_v.at[k], chunk_sem.at[0, k]),
            pltpu.make_async_copy(grads.at[at, :], grads_v.at[k], chunk_sem.at[1, k]),
        )
        for copy in chunk[k]:
            copy.start()
    late = [pltpu.make_async_copy(diag, diag_v, in_sem.at[4])]
    for k in range(NY):
        at = pl.ds(pl.multiple_of(y_at(k) * 512, 512), 512)
        late.append(pltpu.make_async_copy(inv.at[:, at], inv_v.at[k], in_sem.at[5 + k]))
    for k in range(NY):
        at = pl.ds(pl.multiple_of(y_at(NY - k) * 512, 512), 512)
        late.append(pltpu.make_async_copy(train.at[:, at], train_v.at[k], in_sem.at[9 + k]))
    for copy in late:
        copy.start()

    barrier = pltpu.get_barrier_semaphore()
    for k in range(1, NF):
        pl.semaphore_signal(barrier, inc=1, device_id=feat_at(k))
    for k in Y_FAR:
        pl.semaphore_signal(barrier, inc=1, device_id=rows_peer(z, y_at(k)))
    for k in Z_FAR:
        pl.semaphore_signal(barrier, inc=1, device_id=rows_peer(z_at(k), y))

    loads[0].wait()
    loads[1].wait()
    doc, lane = iota((K, K), 0), iota((K, K), 1)
    count_row = jnp.broadcast_to(counts_v[...].astype(F32), (K, K))
    start = jnp.sum(jnp.where(lane < doc, count_row, 0.0), axis=1, keepdims=True)
    count = jnp.sum(jnp.where(lane == doc, count_row, 0.0), axis=1, keepdims=True)
    q = iota((DOCS, NF * NR), 1)
    block = (((q & 31) << 3) | (q >> 5)).astype(F32)
    member[...] = jnp.where((start <= block) & (block < start + count), 1.0, 0.0).astype(BF)
    mine = (r * NF + f).astype(F32)
    owner = jnp.sum(jnp.where(start <= mine, 1.0, 0.0), axis=0, keepdims=True) - 1.0
    same = jnp.where(ids_v[pl.ds(f, 1), :].astype(F32) == owner, 1.0, 0.0)
    keep = jnp.sum(jnp.where(lane == doc, jnp.broadcast_to(same, (K, K)), 0.0), axis=1, keepdims=True)
    columns[0] = jnp.broadcast_to(keep, (K, K))
    columns[1] = jnp.broadcast_to(count, (K, K))
    perms[0] = one_hot_rows(lambda q: ((q >> 2) & 7) * 16 + (q >> 5) * 4 + (q & 3))
    perms[1] = one_hot_rows(lambda q: ((q >> 2) & 3) * 32 + (q >> 4) * 4 + (q & 3))
    perms[2] = one_hot_rows(lambda q: ((q >> 2) & 7) * 16 + (q & 3) * 4 + (q >> 5))

    sends = []

    def send(src, dst, ssem, rsem, device):
        copy = pltpu.make_async_remote_copy(
            src_ref=src, dst_ref=dst, send_sem=ssem, recv_sem=rsem,
            device_id=device, device_id_type=pl.DeviceIdType.MESH,
        )
        copy.start()
        sends.append(copy)
        return copy

    mine_at = pl.ds(pl.multiple_of(c * BLOCK, BLOCK), BLOCK)
    theirs_at = pl.ds(pl.multiple_of((1 - c) * BLOCK, BLOCK), BLOCK)
    from_sib, from_x = {}, {}

    def project(k):
        chunk[k][0].wait()
        pa[k, :, 0:K] = dot(acts_v[k], pin_v[...])
        chunk[k][1].wait()
        pa[k, :, K:2 * K] = dot(grads_v[k], pout_v[...])

    def to_sibling(k):
        from_sib[k] = send(pa.at[k, theirs_at, :], sib.at[k], sib_send.at[k], sib_recv.at[k], sibling)

    def to_owner(k):
        from_sib[k].wait_recv()
        xs[k] = (pa[k, mine_at, :] + sib[k]).astype(X_DT)
        device = {"feat": lax.rem(x + k, NX) * NC + c}
        from_x[k] = send(xs.at[k], xr.at[k], x_send.at[k], x_recv.at[k], device)

    loads[2].wait()
    loads[3].wait()
    project(2)
    pl.semaphore_wait(barrier, NF - 1 + len(Y_FAR) + len(Z_FAR))
    to_sibling(2)
    project(1)
    to_sibling(1)
    to_owner(2)
    project(3)
    to_sibling(3)
    to_owner(1)
    project(0)
    to_sibling(0)
    to_owner(3)
    from_sib[0].wait_recv()
    total = pa[0, mine_at, :] + sib[0]
    for k in (1, 3, 2):
        from_x[k].wait_recv()
        total = total + xr[k].astype(F32)

    xin = total[:, 0:K].astype(BF)
    gmask = jnp.where(columns[0] > 0.5, total[:, K:2 * K], 0.0).astype(BF)
    turned = dot_nt(perms[0], gmask).astype(BF)
    blocksum = dot(turned, xin).astype(BF)
    for k in range(NY):
        s1[k] = blocksum[32 * k:32 * k + 32]
    got = {}
    for k in Y_FAR:
        got[k] = send(s1.at[y_at(k)], r1.at[y], b1_send.at[k], b1_recv.at[k], rows_peer(z, y_at(k)))
    r1[y] = s1[y]
    for k in Y_NEAR:
        got[k].wait_recv()
    second = dot(perms[1], r1[...].reshape(K, K)).astype(BF)
    for k in range(NZ):
        s2[k] = second[16 * k:16 * k + 16]
    for k in Z_FAR:
        got[k] = send(s2.at[z_at(k)], r2.at[z], b2_send.at[k], b2_recv.at[k], rows_peer(z_at(k), y))
    r2[z] = s2[z]
    for k in Z_NEAR:
        got[k].wait_recv()
    third = dot(perms[2], r2[...].reshape(K, K)).astype(BF)
    ag_at = pl.ds(pl.multiple_of(f * NR, NR), NR)
    for k in range(4):
        ags[k] = third[NR * k:NR * k + NR]
    for k in F_FAR:
        got[k] = send(ags, ag.at[:, ag_at, :], ag_send.at[k], ag_recv.at[k], feat_at(k))
    for k in range(4):
        ag[k, ag_at, :] = third[NR * k:NR * k + NR]
    for copy in late:
        copy.wait()
    for k in F_FAR[::-1]:
        got[k].wait_recv()

    for k in range(4):
        dg[:, K * k:K * k + K] = (dot(member[...], ag[k]) / columns[1]).astype(BF)

    for k in Y_FAR:
        s3[k] = dot(dg[...], inv_v[k]).astype(BF)
        got[k] = send(s3.at[k], r3.at[k], c1_send.at[k], c1_recv.at[k], rows_peer(z, y_at(k)))
    own[...] = dot(dg[...], inv_v[0])
    for k in range(4):
        at = slice(K * k, K * k + K)
        own[:, at] += jnp.where(z == f, dg[:, at].astype(F32) * diag_v[k:k + 1, :], 0.0)
    for k in Y_NEAR:
        got[k].wait_recv()
    own[...] = own[...] + r3[1].astype(F32) + r3[3].astype(F32) + r3[2].astype(F32)
    s4[...] = own[...].astype(BF)
    for k in Z_FAR:
        at = pl.ds(pl.multiple_of(z_at(k) * 16, 16), 16)
        got[k] = send(s4.at[at, :], r4.at[k], c2_send.at[k], c2_recv.at[k], rows_peer(z_at(k), y))
    here = pl.ds(pl.multiple_of(z * 16, 16), 16)
    piece = own[here, :]
    for k in Z_NEAR:
        got[k].wait_recv()
        piece = piece + r4[k].astype(F32)
    pc[0, here, :] = piece.astype(BF)

    gather = {}

    def forward(at, j):
        for k in Y_FAR:
            copy = send(
                pc.at[0, at, :], pc.at[k, at, :], p2_send.at[j, k], p2_recv.at[k], rows_peer(z, y_at(k))
            )
        return copy

    for k in Z_FAR:
        gather[k] = send(
            pc.at[0, here, :], pc.at[0, here, :], p1_send.at[k], p1_recv.at[k], rows_peer(z_at(k), y)
        )
    forward(here, 0)
    for k in Z_NEAR:
        gather[k].wait_recv()
        forward(pl.ds(pl.multiple_of(z_at(NZ - k) * 16, 16), 16), k)
    acc[...] = dot_nt(pc[0], train_v[0])
    for k in Y_NEAR:
        pltpu.make_async_copy(pc.at[k], pc.at[k], p2_recv.at[k]).wait()
        acc[...] += dot_nt(pc[k], train_v[k])

    for k in range(NF):
        s5[k] = acc[16 * k:16 * k + 16, :].astype(D_DT)
    for k in F_FAR:
        got[k] = send(s5.at[lax.rem(f + k, NF)], r5.at[k], d_send.at[k], d_recv.at[k], feat_at(k))
    scores = acc[pl.ds(pl.multiple_of(f * 16, 16), 16), :]
    for k in F_FAR[::-1]:
        got[k].wait_recv()
        scores = scores + r5[k].astype(F32)
    out[...] = scores
    for copy in sends:
        copy.wait_send()


def per_device(acts, grads_out, proj_in, proj_out, doc_ids, block_counts, inverse_dense, inverse_diag, train_grads):
    def vmem(*shape, dtype=BF):
        return pltpu.VMEM(shape, dtype)

    dma = pltpu.SemaphoreType.DMA
    scratch = [
        vmem(4, 256, 2048), vmem(4, 256, 2048), vmem(2048, K), vmem(2048, K),
        vmem(8, 128, dtype=I32), vmem(1, 128, dtype=I32),
        vmem(4, 512, 512), vmem(4, 128, dtype=F32), vmem(4, 512, 512),
        vmem(DOCS, 256), vmem(3, K, K), vmem(2, K, K, dtype=F32),
        vmem(4, 256, 256, dtype=F32), vmem(4, 128, 256, dtype=F32),
        vmem(4, 128, 256, dtype=X_DT), vmem(4, 128, 256, dtype=X_DT),
        vmem(4, 32, K), vmem(4, 32, K), vmem(8, 16, K), vmem(8, 16, K),
        vmem(4, 32, K), vmem(4, 256, K), vmem(128, 512),
        vmem(4, 128, 512), vmem(4, 128, 512), vmem(128, 512, dtype=F32),
        vmem(128, 512), vmem(8, 16, 512), vmem(4, 128, 512), vmem(128, 512, dtype=F32),
        vmem(8, 16, 512, dtype=D_DT), vmem(8, 16, 512, dtype=D_DT),
        dma((13,)), dma((2, 4)),
        dma((4,)), dma((4,)), dma((4,)), dma((4,)), dma((4,)), dma((4,)), dma((8,)), dma((8,)),
        dma((8,)), dma((8,)), dma((4,)), dma((4,)), dma((8,)), dma((8,)), dma((8,)), dma((8,)),
        dma((8, 4)), dma((4,)), dma((8,)), dma((8,)),
    ]
    hbm = pl.BlockSpec(memory_space=pl.ANY)
    return pl.pallas_call(
        kernel,
        out_shape=jax.ShapeDtypeStruct((16, 512), F32),
        in_specs=[hbm] * 9,
        out_specs=pl.BlockSpec(memory_space=pltpu.VMEM),
        scratch_shapes=scratch,
        compiler_params=pltpu.CompilerParams(
            collective_id=0, has_side_effects=True, vmem_limit_bytes=60 * 1024 * 1024
        ),
        name="influence",
    )(
        acts, grads_out, proj_in, proj_out,
        doc_ids.reshape(8, 128), block_counts.reshape(1, 128),
        inverse_dense, inverse_diag.reshape(4, 128), train_grads,
    )


def solution(mesh):
    in_specs = (
        P("rows", "feat"),
        P("rows", "feat"),
        P("feat", None),
        P("feat", None),
        P("rows"),
        P(),
        P("rows", "feat"),
        P("rows"),
        P("rows", "feat"),
    )
    return jax.shard_map(
        per_device, mesh=mesh, in_specs=in_specs, out_specs=P("feat", "rows"), check_vma=False
    )
```

time: 143 us -> 61.6 us (0.43)
  blocking collectives: 79.3 us -> 0 us
  Pallas kernels: 0 us -> 60.1 us
  waiting for transfers between devices: 31 us -> 0 us
  starting transfers between devices: 17 us -> 0 us
  matrix products: 8.97 us -> 0 us
  other arithmetic: 2.48 us -> 0 us
  local copies, waits for them, and re-layouts: 3.38 us -> 1.38 us
    all_to_all x3 -> x0, blocking collectives: 66.3 us -> none  [the longest x2 45.2 us: sent_and_summed(): lax.all_to_all(blocks, axis, split_axis=0, concat_axis=0, tiled=True)]
    pallas_call x0 -> x1, Pallas kernels: none -> 60.1 us  [per_device(): pl.pallas_call(kernel, out_shape=jax.ShapeDtypeStruct((16, 512), F32), in...]
    all_to_all x2 -> x0, waiting for transfers between devices: 31 us -> none  [the longest x1 16.7 us: per_device(): lax.all_to_all(local_sums, 'rows', split_axis=1, concat_axis=0, tiled=True)]
    all_to_all x2 -> x0, starting transfers between devices: 17 us -> none  [the longest x1 10.3 us: per_device(): lax.all_to_all(local_sums, 'rows', split_axis=1, concat_axis=0, tiled=True)]
    all_gather x1 -> x0, blocking collectives: 13 us -> none  [in_one_piece(): lax.all_gather(both, axis, axis=dim, tiled=True)]
    dot_general x6 -> x0, matrix products: 8.97 us -> none  [the longest x1 3.97 us: per_device(): part_in = jnp.dot(acts, proj_in, preferred_element_type=jnp.float32)]
  transfers between devices with their start and end apart: 2 -> 0, of which waited for: 2 -> 0; matrix products, arithmetic and copies ran while one was open for 0% -> 0% of each run, Pallas kernels for 0% -> 0%
where the time goes in v1:
time: 61.6 us; the launch traced here: 61.5 us
  Pallas kernels  60.1 us (98%)
  local copies, waits for them, and re-layouts  1.38 us (2%)
    pallas_call x1, Pallas kernels, per_device(): pl.pallas_call(kernel, out_shape=jax.ShapeDtypeStruct((16, 512), F32), in...  60.1 us
    unnamed x1, local copies, waits for them, and re-layouts  1.38 us

profile of v1, /device:TPU:1, one launch (start us, length us, event | category | flops | bytes accessed | tf_op | source)
XLA Modules:
  0.0 61.5 jit_solution(17710544095522248046)
XLA Ops:
  0.0 60.1 %influence.1 = f32[16,512]{1,0:T(8,128)} custom-call(bf16[1024,2048]{1,0:T(8,128)(2,1)} %acts.1, bf16[1024,2048]{1,0:T(8,128)(2,1)} %grads.1, bf16[2048,128]{1,0:T(8,128)(2,1)} %pin.1, bf16[2048,128]{1,0:T(8,128)(2,1)} %pout.1, s32[8,128]{1,0:T(8,128)} %bitcast.3, s32[1,128]{1,0:T(1,128)} %bitcast.5, bf16[512,2048]{1,0:T(8,128)(2,1)} %inv.1, ...), custom_call_target="tpu_custom_call" | custom-call | tf_op jit(solution)/shard_map/influence/pallas_call | solution.py:294
  60.1 1.4 %copy.11 = f32[16,512]{1,0:T(8,128)} copy(f32[16,512]{1,0:T(8,128)} %influence.1) | data formatting | bytes 65536

commit v2 on v1

v2 whole, which is shorter than its diff:
```python
import jax
import jax.numpy as jnp
from jax import lax
from jax.experimental import pallas as pl
from jax.experimental.pallas import tpu as pltpu
from jax.sharding import PartitionSpec as P

BF = jnp.bfloat16
F32 = jnp.float32
I32 = jnp.int32

NX, NC, NY, NZ = 4, 2, 4, 8
NF = NX * NC
NR = NZ * NY
BLOCK = 128
K = 128
DOCS = 128
Y_FAR = (2, 1, 3)
Y_NEAR = (1, 3, 2)
Z_FAR = (4, 3, 5, 2, 6, 1, 7)
Z_NEAR = (1, 7, 2, 6, 3, 5, 4)
F_FAR = (4, 5, 3, 2, 6, 7, 1)
X_FAR = (2, 1, 3)
R_FAR = sorted(
    ((dz, dy) for dz in range(NZ) for dy in range(NY) if dz or dy),
    key=lambda d: -min(d[0], NZ - d[0]) - min(d[1], NY - d[1]),
)
X_DT = BF
B_DT = BF
D_DT = BF


def iota(shape, dim):
    return lax.broadcasted_iota(I32, shape, dim)


def one_hot_rows(source_of):
    q = iota((K, K), 0)
    return (iota((K, K), 1) == source_of(q)).astype(F32).astype(BF)


def dot(a, b):
    return jnp.dot(a, b, preferred_element_type=F32)


def dot_nt(a, b):
    return lax.dot_general(a, b, (((1,), (1,)), ((), ())), preferred_element_type=F32)


def kernel(
    acts, grads, pin, pout, ids, counts, inv, diag, train,
    out,
    tokens_v, proj_v, ids_v, counts_v, inv_v, diag_v, train_v,
    member, perms, columns,
    pa, sib, xs, xr, s1, r1, ag, dg, s3, r3, own, s4, r4, pc, acc, s5, r5,
    in_sem, chunk_sem, plane,
    sib_send, sib_recv, x_send, x_recv, b1_send, b1_recv,
    ag_send, ag_recv, c1_send, c1_recv, c2_send, c2_recv, p1_send, p1_recv,
    p2_send, p2_recv, d_send, d_recv,
):
    f = lax.axis_index("feat")
    r = lax.axis_index("rows")
    x, c = f // NC, f % NC
    z, y = r // NY, r % NY

    def feat_at(k):
        return {"feat": lax.rem(f + k, NF)}

    def y_at(k):
        return lax.rem(y + k, NY)

    def z_at(k):
        return lax.rem(z + k, NZ)

    def rows_peer(zp, yp):
        return {"rows": zp * NY + yp}

    sibling = {"feat": x * NC + (1 - c)}

    projections = [
        pltpu.make_async_copy(pin, proj_v.at[0], in_sem.at[0]),
        pltpu.make_async_copy(pout, proj_v.at[1], in_sem.at[0]),
    ]
    for copy in projections:
        copy.start()

    def ahead(j):
        return jnp.where(j == 0, 2, jnp.where(j == 1, 1, jnp.where(j == 2, 3, 0)))

    def chunk(j):
        at = pl.ds(pl.multiple_of(lax.rem(x + ahead(j), NX) * 256, 256), 256)
        return (
            pltpu.make_async_copy(acts.at[at, :], tokens_v.at[j, 0], chunk_sem.at[j]),
            pltpu.make_async_copy(grads.at[at, :], tokens_v.at[j, 1], chunk_sem.at[j]),
        )

    for j in range(NX):
        for copy in chunk(j):
            copy.start()
    small = [
        pltpu.make_async_copy(counts, counts_v, in_sem.at[1]),
        pltpu.make_async_copy(ids, ids_v, in_sem.at[2]),
        pltpu.make_async_copy(diag, diag_v, in_sem.at[3]),
    ]
    late = []
    for k in range(NY):
        at = pl.ds(pl.multiple_of(y_at(k) * 512, 512), 512)
        late.append(pltpu.make_async_copy(inv.at[:, at], inv_v.at[k], in_sem.at[4]))
    for k in range(NY):
        at = pl.ds(pl.multiple_of(y_at(NY - k) * 512, 512), 512)
        late.append(pltpu.make_async_copy(train.at[:, at], train_v.at[k], in_sem.at[5]))

    barrier = pltpu.get_barrier_semaphore()
    for k in range(1, NF):
        pl.semaphore_signal(barrier, inc=1, device_id=feat_at(k))
    for k in Z_FAR:
        pl.semaphore_signal(barrier, inc=1, device_id=rows_peer(z_at(k), y))
    for k in Y_FAR:
        pl.semaphore_signal(barrier, inc=1, device_id=rows_peer(z, y_at(k)))

    sent = []

    def remote(src, dst, ssem, rsem, device):
        return pltpu.make_async_remote_copy(
            src_ref=src, dst_ref=dst, send_sem=ssem, recv_sem=rsem,
            device_id=device, device_id_type=pl.DeviceIdType.MESH,
        )

    def send(*args):
        copy = remote(*args)
        copy.start()
        return copy

    def wait_all(ref, sem):
        pltpu.make_async_copy(ref, ref, sem).wait()

    def finish():
        for ref, sem in sent:
            wait_all(ref, sem)

    mine_at = pl.ds(pl.multiple_of(c * BLOCK, BLOCK), BLOCK)
    theirs_at = pl.ds(pl.multiple_of((1 - c) * BLOCK, BLOCK), BLOCK)

    def to_sibling(j):
        return remote(pa.at[j, theirs_at, :], sib.at[j], sib_send, sib_recv.at[j], sibling)

    def to_owner(j):
        device = {"feat": lax.rem(x + ahead(j), NX) * NC + c}
        return remote(xs.at[j], xr.at[j], x_send, x_recv, device)

    wait_all(proj_v, in_sem.at[0])

    def step(j, carry):
        wait_all(tokens_v.at[j], chunk_sem.at[j])
        pa[j, :, 0:K] = dot(tokens_v[j, 0], proj_v[0])
        pa[j, :, K:2 * K] = dot(tokens_v[j, 1], proj_v[1])

        @pl.when(j == 0)
        def _():
            pl.semaphore_wait(barrier, NF + NY + NZ - 3)
            for k in Y_FAR:
                pl.semaphore_signal(plane, inc=1, device_id=rows_peer(z, y_at(k)))

        to_sibling(j).start()

        @pl.when(j > 0)
        def _():
            to_sibling(j - 1).wait_recv()
            xs[j - 1] = (pa[j - 1, mine_at, :] + sib[j - 1]).astype(X_DT)
            to_owner(j - 1).start()

        return carry

    lax.fori_loop(0, NX, step, 0)
    for copy in small + late:
        copy.start()
    sent += [(sib, sib_send), (xs.at[0:NX - 1], x_send)]
    to_sibling(NX - 1).wait_recv()

    for copy in small:
        copy.wait()
    doc, lane = iota((K, K), 0), iota((K, K), 1)
    count_row = jnp.broadcast_to(counts_v[...].astype(F32), (K, K))
    start = jnp.sum(jnp.where(lane < doc, count_row, 0.0), axis=1, keepdims=True)
    count = jnp.sum(jnp.where(lane == doc, count_row, 0.0), axis=1, keepdims=True)
    q = iota((DOCS, NF * NR), 1)
    block = (((q & 31) << 3) | (q >> 5)).astype(F32)
    member[...] = jnp.where((start <= block) & (block < start + count), 1.0, 0.0).astype(BF)
    mine = (r * NF + f).astype(F32)
    owner = jnp.sum(jnp.where(start <= mine, 1.0, 0.0), axis=0, keepdims=True) - 1.0
    same = jnp.where(ids_v[pl.ds(f, 1), :].astype(F32) == owner, 1.0, 0.0)
    keep = jnp.sum(jnp.where(lane == doc, jnp.broadcast_to(same, (K, K)), 0.0), axis=1, keepdims=True)
    columns[0] = jnp.broadcast_to(keep, (K, K))
    columns[1] = jnp.broadcast_to(count, (K, K))
    perms[0] = one_hot_rows(lambda q: (q & 31) * 4 + (q >> 5))

    total = pa[NX - 1, mine_at, :] + sib[NX - 1]
    wait_all(xr.at[0:NX - 1], x_recv)
    for j in range(NX - 1):
        total = total + xr[j].astype(F32)

    gmask = jnp.where(columns[0] > 0.5, total[:, K:2 * K], 0.0)
    blocksum = jnp.dot(
        gmask.T, total[:, 0:K], precision=lax.Precision.HIGHEST, preferred_element_type=F32
    )
    s1[...] = blocksum.astype(B_DT).reshape(NR, 4, K)
    got = {}
    pl.semaphore_wait(plane, NY - 1)
    for dz, dy in R_FAR:
        there = z_at(dz) * NY + y_at(dy)
        send(s1.at[there], r1.at[r], b1_send, b1_recv, {"rows": there})
    sent.append((s1.at[0:NR - 1], b1_send))
    r1[r] = s1[r]
    wait_all(r1.at[0:NR - 1], b1_recv)

    turned = dot(perms[0], r1[...].reshape(K, K).astype(BF)).astype(BF)
    ag_at = pl.ds(pl.multiple_of(f * NR, NR), NR)
    for k in range(4):
        ag[k, ag_at, :] = turned[NR * k:NR * k + NR]

    def share(at, k, device):
        return send(ag.at[:, at, :], ag.at[:, at, :], ag_send, ag_recv.at[k], device)

    for k in X_FAR:
        got[k] = share(ag_at, k, feat_at(NC * k))
    share(ag_at, 0, sibling)
    for k in X_FAR[::-1]:
        got[k].wait_recv()
        at = pl.ds(pl.multiple_of(lax.rem(f + NF - NC * k, NF) * NR, NR), NR)
        share(at, 0, sibling)
    sent.append((ag.at[:, 0:(NF - 1) * NR, :], ag_send))
    wait_all(inv_v, in_sem.at[4])
    wait_all(train_v, in_sem.at[5])
    wait_all(ag.at[:, 0:NX * NR, :], ag_recv.at[0])

    for k in range(4):
        dg[:, K * k:K * k + K] = (dot(member[...], ag[k]) / columns[1]).astype(BF)

    for k in Y_FAR:
        s3[k] = dot(dg[...], inv_v[k]).astype(BF)
        send(s3.at[k], r3.at[k], c1_send, c1_recv, rows_peer(z, y_at(k)))
    sent.append((s3.at[1:NY], c1_send))
    own[...] = dot(dg[...], inv_v[0])
    for k in range(4):
        at = slice(K * k, K * k + K)
        own[:, at] += jnp.where(z == f, dg[:, at].astype(F32) * diag_v[k:k + 1, :], 0.0)
    wait_all(r3.at[1:NY], c1_recv)
    own[...] = own[...] + r3[1].astype(F32) + r3[3].astype(F32) + r3[2].astype(F32)
    s4[...] = own[...].astype(BF)
    for k in Z_FAR:
        at = pl.ds(pl.multiple_of(z_at(k) * 16, 16), 16)
        send(s4.at[at, :], r4.at[k], c2_send, c2_recv, rows_peer(z_at(k), y))
    sent.append((s4.at[0:16 * (NZ - 1), :], c2_send))
    here = pl.ds(pl.multiple_of(z * 16, 16), 16)
    piece = own[here, :]
    wait_all(r4.at[1:NZ], c2_recv)
    for k in Z_NEAR:
        piece = piece + r4[k].astype(F32)
    pc[0, here, :] = piece.astype(BF)

    gather = {}

    def forward(at):
        for k in Y_FAR:
            send(pc.at[0, at, :], pc.at[k, at, :], p2_send, p2_recv.at[k], rows_peer(z, y_at(k)))

    for k in Z_FAR:
        gather[k] = send(
            pc.at[0, here, :], pc.at[0, here, :], p1_send, p1_recv.at[k], rows_peer(z_at(k), y)
        )
    forward(here)
    for k in Z_NEAR:
        gather[k].wait_recv()
        forward(pl.ds(pl.multiple_of(z_at(NZ - k) * 16, 16), 16))
    sent += [(pc.at[0, 0:16 * (NZ - 1), :], p1_send), (pc.at[0:NY - 1], p2_send)]
    acc[...] = dot_nt(pc[0], train_v[0])
    for k in Y_NEAR:
        wait_all(pc.at[k], p2_recv.at[k])
        acc[...] += dot_nt(pc[k], train_v[k])

    for k in range(NF):
        s5[k] = acc[16 * k:16 * k + 16, :].astype(D_DT)
    for k in F_FAR:
        send(s5.at[lax.rem(f + k, NF)], r5.at[k], d_send, d_recv, feat_at(k))
    sent.append((s5.at[1:NF], d_send))
    scores = acc[pl.ds(pl.multiple_of(f * 16, 16), 16), :]
    wait_all(r5.at[1:NF], d_recv)
    for k in F_FAR[::-1]:
        scores = scores + r5[k].astype(F32)
    out[...] = scores
    finish()


def per_device(acts, grads_out, proj_in, proj_out, doc_ids, block_counts, inverse_dense, inverse_diag, train_grads):
    def vmem(*shape, dtype=BF):
        return pltpu.VMEM(shape, dtype)

    dma = pltpu.SemaphoreType.DMA
    scratch = [
        vmem(4, 2, 256, 2048), vmem(2, 2048, K),
        vmem(8, 128, dtype=I32), vmem(1, 128, dtype=I32),
        vmem(4, 512, 512), vmem(4, 128, dtype=F32), vmem(4, 512, 512),
        vmem(DOCS, 256), vmem(1, K, K), vmem(2, K, K, dtype=F32),
        vmem(4, 256, 256, dtype=F32), vmem(4, 128, 256, dtype=F32),
        vmem(4, 128, 256, dtype=X_DT), vmem(4, 128, 256, dtype=X_DT),
        vmem(NR, 4, K, dtype=B_DT), vmem(NR, 4, K, dtype=B_DT),
        vmem(4, 256, K), vmem(128, 512),
        vmem(4, 128, 512), vmem(4, 128, 512), vmem(128, 512, dtype=F32),
        vmem(128, 512), vmem(8, 16, 512), vmem(4, 128, 512), vmem(128, 512, dtype=F32),
        vmem(8, 16, 512, dtype=D_DT), vmem(8, 16, 512, dtype=D_DT),
        dma((6,)), dma((NX,)), pltpu.SemaphoreType.REGULAR,
        dma(()), dma((NX,)), dma(()), dma(()), dma(()), dma(()), dma(()), dma((NX,)),
        dma(()), dma(()), dma(()), dma(()), dma(()), dma((NZ,)), dma(()), dma((NY,)),
        dma(()), dma(()),
    ]
    hbm = pl.BlockSpec(memory_space=pl.ANY)
    return pl.pallas_call(
        kernel,
        out_shape=jax.ShapeDtypeStruct((16, 512), F32),
        in_specs=[hbm] * 9,
        out_specs=pl.BlockSpec(memory_space=pltpu.VMEM),
        scratch_shapes=scratch,
        compiler_params=pltpu.CompilerParams(
            collective_id=0, has_side_effects=True, vmem_limit_bytes=60 * 1024 * 1024
        ),
        name="influence",
    )(
        acts, grads_out, proj_in, proj_out,
        doc_ids.reshape(8, 128), block_counts.reshape(1, 128),
        inverse_dense, inverse_diag.reshape(4, 128), train_grads,
    )


def solution(mesh):
    in_specs = (
        P("rows", "feat"),
        P("rows", "feat"),
        P("feat", None),
        P("feat", None),
        P("rows"),
        P(),
        P("rows", "feat"),
        P("rows"),
        P("rows", "feat"),
    )
    return jax.shard_map(
        per_device, mesh=mesh, in_specs=in_specs, out_specs=P("feat", "rows"), check_vma=False
    )
```

time: 61.6 us -> 59.9 us (0.972)
  Pallas kernels: 60.1 us -> 58.4 us
    pallas_call x1, Pallas kernels: 60.1 us -> 58.4 us  [per_device(): pl.pallas_call(kernel, out_shape=jax.ShapeDtypeStruct((16, 512), F32), in...]
where the time goes in v2:
time: 59.9 us; the launch traced here: 59.8 us
  Pallas kernels  58.4 us (97%)
  local copies, waits for them, and re-layouts  1.38 us (2%)
    pallas_call x1, Pallas kernels, per_device(): pl.pallas_call(kernel, out_shape=jax.ShapeDtypeStruct((16, 512), F32), in...  58.4 us
    unnamed x1, local copies, waits for them, and re-layouts  1.38 us

profile of v2, /device:TPU:1, one launch (start us, length us, event | category | flops | bytes accessed | tf_op | source)
XLA Modules:
  0.0 59.8 jit_solution(10712771460438245814)
XLA Ops:
  0.0 58.4 %influence.1 = f32[16,512]{1,0:T(8,128)} custom-call(bf16[1024,2048]{1,0:T(8,128)(2,1)} %acts.1, bf16[1024,2048]{1,0:T(8,128)(2,1)} %grads.1, bf16[2048,128]{1,0:T(8,128)(2,1)} %pin.1, bf16[2048,128]{1,0:T(8,128)(2,1)} %pout.1, s32[8,128]{1,0:T(8,128)} %bitcast.3, s32[1,128]{1,0:T(1,128)} %bitcast.5, bf16[512,2048]{1,0:T(8,128)(2,1)} %inv.1, ...), custom_call_target="tpu_custom_call" | custom-call | tf_op jit(solution)/shard_map/influence/pallas_call | solution.py:317
  58.4 1.4 %copy.11 = f32[16,512]{1,0:T(8,128)} copy(f32[16,512]{1,0:T(8,128)} %influence.1) | data formatting | bytes 65536

commit v3 on v2

--- a/solution.py
+++ b/solution.py
@@ -221,17 +221,12 @@
     def share(at, k, device):
         return send(ag.at[:, at, :], ag.at[:, at, :], ag_send, ag_recv.at[k], device)
 
-    for k in X_FAR:
-        got[k] = share(ag_at, k, feat_at(NC * k))
-    share(ag_at, 0, sibling)
-    for k in X_FAR[::-1]:
-        got[k].wait_recv()
-        at = pl.ds(pl.multiple_of(lax.rem(f + NF - NC * k, NF) * NR, NR), NR)
-        share(at, 0, sibling)
+    for k in F_FAR:
+        share(ag_at, 0, feat_at(k))
     sent.append((ag.at[:, 0:(NF - 1) * NR, :], ag_send))
     wait_all(inv_v, in_sem.at[4])
     wait_all(train_v, in_sem.at[5])
-    wait_all(ag.at[:, 0:NX * NR, :], ag_recv.at[0])
+    wait_all(ag.at[:, 0:(NF - 1) * NR, :], ag_recv.at[0])
 
     for k in range(4):
         dg[:, K * k:K * k + K] = (dot(member[...], ag[k]) / columns[1]).astype(BF)
@@ -264,7 +259,7 @@
         for k in Y_FAR:
             send(pc.at[0, at, :], pc.at[k, at, :], p2_send, p2_recv.at[k], rows_peer(z, y_at(k)))
 
-    for k in Z_FAR:
+    for k in Z_NEAR:
         gather[k] = send(
             pc.at[0, here, :], pc.at[0, here, :], p1_send, p1_recv.at[k], rows_peer(z_at(k), y)
         )

time: 59.9 us -> 58.9 us (0.983)
  Pallas kernels: 58.4 us -> 57.4 us
    pallas_call x1, Pallas kernels: 58.4 us -> 57.4 us  [per_device(): pl.pallas_call(kernel, out_shape=jax.ShapeDtypeStruct((16, 512), F32), in...]
where the time goes in v3:
time: 58.9 us; the launch traced here: 58.8 us
  Pallas kernels  57.4 us (97%)
  local copies, waits for them, and re-layouts  1.38 us (2%)
    pallas_call x1, Pallas kernels, per_device(): pl.pallas_call(kernel, out_shape=jax.ShapeDtypeStruct((16, 512), F32), in...  57.4 us
    unnamed x1, local copies, waits for them, and re-layouts  1.38 us

profile of v3, /device:TPU:1, one launch (start us, length us, event | category | flops | bytes accessed | tf_op | source)
XLA Modules:
  0.0 58.8 jit_solution(4342649334453523034)
XLA Ops:
  0.0 57.4 %influence.1 = f32[16,512]{1,0:T(8,128)} custom-call(bf16[1024,2048]{1,0:T(8,128)(2,1)} %acts.1, bf16[1024,2048]{1,0:T(8,128)(2,1)} %grads.1, bf16[2048,128]{1,0:T(8,128)(2,1)} %pin.1, bf16[2048,128]{1,0:T(8,128)(2,1)} %pout.1, s32[8,128]{1,0:T(8,128)} %bitcast.3, s32[1,128]{1,0:T(1,128)} %bitcast.5, bf16[512,2048]{1,0:T(8,128)(2,1)} %inv.1, ...), custom_call_target="tpu_custom_call" | custom-call | tf_op jit(solution)/shard_map/influence/pallas_call | solution.py:312
  57.4 1.4 %copy.11 = f32[16,512]{1,0:T(8,128)} copy(f32[16,512]{1,0:T(8,128)} %influence.1) | data formatting | bytes 65536

commit v4 on v3

--- a/solution.py
+++ b/solution.py
@@ -102,6 +102,8 @@
         pltpu.make_async_copy(ids, ids_v, in_sem.at[2]),
         pltpu.make_async_copy(diag, diag_v, in_sem.at[3]),
     ]
+    for copy in small:
+        copy.start()
     late = []
     for k in range(NY):
         at = pl.ds(pl.multiple_of(y_at(k) * 512, 512), 512)
@@ -172,7 +174,7 @@
         return carry
 
     lax.fori_loop(0, NX, step, 0)
-    for copy in small + late:
+    for copy in late:
         copy.start()
     sent += [(sib, sib_send), (xs.at[0:NX - 1], x_send)]
     to_sibling(NX - 1).wait_recv()

time: 58.9 us -> 58.3 us (0.990)
  Pallas kernels: 57.4 us -> 56.8 us
    pallas_call x1, Pallas kernels: 57.4 us -> 56.8 us  [per_device(): pl.pallas_call(kernel, out_shape=jax.ShapeDtypeStruct((16, 512), F32), in...]
where the time goes in v4:
time: 58.3 us; the launch traced here: 58.1 us
  Pallas kernels  56.8 us (97%)
  local copies, waits for them, and re-layouts  1.38 us (2%)
    pallas_call x1, Pallas kernels, per_device(): pl.pallas_call(kernel, out_shape=jax.ShapeDtypeStruct((16, 512), F32), in...  56.8 us
    unnamed x1, local copies, waits for them, and re-layouts  1.38 us

profile of v4, /device:TPU:1, one launch (start us, length us, event | category | flops | bytes accessed | tf_op | source)
XLA Modules:
  0.0 58.1 jit_solution(16789774186941907537)
XLA Ops:
  0.0 56.8 %influence.1 = f32[16,512]{1,0:T(8,128)} custom-call(bf16[1024,2048]{1,0:T(8,128)(2,1)} %acts.1, bf16[1024,2048]{1,0:T(8,128)(2,1)} %grads.1, bf16[2048,128]{1,0:T(8,128)(2,1)} %pin.1, bf16[2048,128]{1,0:T(8,128)(2,1)} %pout.1, s32[8,128]{1,0:T(8,128)} %bitcast.3, s32[1,128]{1,0:T(1,128)} %bitcast.5, bf16[512,2048]{1,0:T(8,128)(2,1)} %inv.1, ...), custom_call_target="tpu_custom_call" | custom-call | tf_op jit(solution)/shard_map/influence/pallas_call | solution.py:314
  56.8 1.4 %copy.11 = f32[16,512]{1,0:T(8,128)} copy(f32[16,512]{1,0:T(8,128)} %influence.1) | data formatting | bytes 65536
